TPU v7x, 128 devices: a whole 4x4x4 slice. The times are simulated.
128 devices in a mesh: section: 16 (over y_lo, x, core), tensor: 8 (over y_hi, z).
Axes of the slice: x: 4, y: 4 (y_hi: 2, y_lo: 2; y = y_hi * 2 + y_lo), z: 4, core: 2. Of those that a mesh axis runs over, the one named last changes fastest.
Arguments:
- key_weight: bfloat16 [16, 8192, 1024], P('section', None, 'tensor'), may hold values from -0.0625 to 0.0625
- value_weight: bfloat16 [16, 8192, 1024], P('section', None, 'tensor'), may hold values from -0.0625 to 0.0625
- norm_gain: bfloat16 [16, 8192], P('section'), may hold values from 0.25 to 1.75
Outputs:
- scaled: bfloat16 [16, 8192, 2048], P(None, ('section', 'tensor'))
- block_scale: float32 [16, 64, 16], P(None, 'section')
All inputs are finite; a program needn't handle non-finite values.
Results may differ from a plain program's by a relative error of at most 0.0056.
Values may be sent and summed in bfloat16 or wider, within the bound.
A program may use at most 128 MiB of HBM per device.

v0:
```python
import jax
import jax.numpy as jnp
from jax import lax
from jax.sharding import PartitionSpec as P

BLOCK = 128


scale_floor = 0.00390625


def route(main_part, side_part):
    lead_count = main_part.shape[0] * main_part.shape[1]
    arrived = (
        lax.all_to_all(
            main_part.reshape((lead_count,) + main_part.shape[2:]),
            ("section", "tensor"),
            split_axis=0,
            concat_axis=0,
            tiled=True,
        ),
        lax.all_to_all(
            side_part.reshape((lead_count,) + side_part.shape[2:]),
            ("section", "tensor"),
            split_axis=0,
            concat_axis=0,
            tiled=True,
        ),
    )
    return (arrived[0].reshape(main_part.shape), arrived[1].reshape(side_part.shape))


def regroup(arrived, layers_here):
    sections_count, ranks_count, row_count, flat_count = arrived.shape
    head_cols = flat_count // (layers_here * 2)
    parted = arrived.reshape(sections_count, ranks_count, row_count, layers_here, 2, head_cols)
    ordered = parted.transpose(0, 3, 2, 4, 1, 5)
    return ordered.reshape(sections_count * layers_here, row_count, 2 * ranks_count * head_cols)


def on_device(key_weight, value_weight, norm_gain):
    layers_here, model_rows, head_cols = key_weight.shape
    sections_count = lax.axis_size("section")
    ranks_count = lax.axis_size("tensor")
    row_share = model_rows // (sections_count * ranks_count)
    col_count = 2 * head_cols
    stacked = jnp.concatenate([key_weight, value_weight], axis=2)
    folded = (norm_gain.astype(jnp.float32)[:, :, None] * stacked.astype(jnp.float32)).astype(
        jnp.bfloat16
    )
    folded = lax.optimization_barrier(folded).astype(jnp.float32)
    col_blocks = col_count // BLOCK
    blocks = folded.reshape(layers_here, model_rows // BLOCK, BLOCK, col_blocks, BLOCK)
    local_scale = jnp.maximum(jnp.max(jnp.abs(blocks), axis=(2, 4)), scale_floor)
    scaled_here = (
        (blocks / local_scale[:, :, None, :, None])
        .astype(jnp.bfloat16)
        .reshape(layers_here, model_rows, col_count)
    )
    section_blocks = model_rows // sections_count // BLOCK
    scale_rows = local_scale.reshape(
        layers_here, sections_count, section_blocks, col_blocks
    ).transpose(1, 2, 0, 3)
    scale_rows = scale_rows.reshape(sections_count, 1, section_blocks, layers_here * col_blocks)
    scale_rows = jnp.broadcast_to(
        scale_rows, (sections_count, ranks_count, section_blocks, layers_here * col_blocks)
    ).astype(jnp.bfloat16)
    values_in, scales_in = route(
        scaled_here.transpose(1, 0, 2).reshape(sections_count, ranks_count, row_share, -1),
        scale_rows,
    )
    scaled = regroup(values_in, layers_here)
    block_scale = regroup(scales_in, layers_here).astype(jnp.float32)
    return (scaled, block_scale)


def solution(mesh):
    placed = (P("section", None, "tensor"), P("section", None, "tensor"), P("section", None))
    return jax.shard_map(
        on_device,
        mesh=mesh,
        in_specs=placed,
        out_specs=(P(None, ("section", "tensor"), None), P(None, "section", None)),
        check_vma=False,
    )
```

profile of v0, /device:TPU:1, one launch (start us, length us, event | category | flops | bytes accessed | tf_op | source)
XLA Modules:
  0.0 133.8 jit_solution(16787883959534104412)
XLA Ops:
  0.6 0.8 convert_element_type.67
  1.4 4.9 %multiply_convert_fusion = bf16[1,8192,256]{2,1,0:T(8,128)(2,1)S(1)} fusion(bf16[1,8192,128]{2,1,0:T(8,128)(2,1)} %param.4, bf16[1,8192,128]{2,1,0:T(8,128)(2,1)} %param.3, f32[8192]{0:T(1024)S(1)} %bitcast.25), kind=kLoop, calls=%fused_computation.1 | loop fusion | flops 12582912 | bytes 8421376 | tf_op jit(solution)/shard_map/convert_element_type | solution.py:48
  6.4 0.0 copy-start
  6.4 2.0 %copy-done = bf16[1,8192,256]{2,1,0:T(8,128)(2,1)} copy-done((bf16[1,8192,256]{2,1,0:T(8,128)(2,1)}, bf16[1,8192,256]{2,1,0:T(8,128)(2,1)S(1)}, u32[]{:S(2)}) %copy-start) | copy-done | bytes 4194328
  8.4 4.0 %convert_abs_fusion = f32[1,8192,256]{2,1,0:T(8,128)} fusion(bf16[1,8192,256]{2,1,0:T(8,128)(2,1)S(1)} %multiply_convert_fusion), kind=kLoop, calls=%fused_computation.2 | loop fusion | flops 4194304 | bytes 12582912 | tf_op jit(solution)/shard_map/abs | solution.py:54
  12.3 10.8 %abs.18 = f32[64,128,2,128]{3,2,1,0:T(2,128)} reshape(f32[1,8192,256]{2,1,0:T(8,128)} %convert_abs_fusion) | data formatting | bytes 16777216 | tf_op jit(solution)/shard_map/abs | solution.py:54
  23.1 5.7 %reduce_max.9 = f32[64,2]{1,0:T(8,128)S(1)} reduce(f32[64,128,2,128]{3,2,1,0:T(2,128)} %abs.18, f32[]{:T(128)} %constant.0.clone.1), dimensions={1,3}, to_apply=%region_0.0 | reduce | flops 2097024 | bytes 8389124 | tf_op jit(solution)/shard_map/reduce_max | solution.py:54
  28.8 0.1 copy.30
  28.9 0.1 convert_element_type.62
  29.0 0.7 broadcast_in_dim.2.clone
  29.6 11.5 %all-to-all-start.1 = ((bf16[128,4,2]{1,2,0:T(2,128)(2,1)}), bf16[128,4,2]{1,2,0:T(2,128)(2,1)S(1)}, u32[]{:S(2)}, u32[]{:S(2)}) async-start(bf16[128,4,2]{1,2,0:T(2,128)(2,1)} %bitcast.3), calls=%async_computation.1 | async-start | bytes 131072 | tf_op jit(solution)/shard_map/all_to_all | solution.py:22
  41.1 0.1 copy.31
  41.2 0.1 div.15
  41.4 6.0 %divide_convert_fusion = bf16[128,64,256]{2,1,0:T(8,128)(2,1)} fusion(f32[128,256]{1,0:T(8,128)S(1)} %bitcast.22, bf16[128,64,256]{2,1,0:T(8,128)(2,1)} %bitcast.20), kind=kLoop, calls=%fused_computation | loop fusion | flops 6291456 | bytes 8519680 | tf_op jit(solution)/shard_map/convert_element_type | solution.py:57
  47.4 3.1 %all-to-all-done.1 = bf16[128,4,2]{1,2,0:T(2,128)(2,1)S(1)} async-done(((bf16[128,4,2]{1,2,0:T(2,128)(2,1)}), bf16[128,4,2]{1,2,0:T(2,128)(2,1)S(1)}, u32[]{:S(2)}, u32[]{:S(2)}) %all-to-all-start.1) | async-done | bytes 2080 | tf_op jit(solution)/shard_map/all_to_all | solution.py:22
  50.5 7.2 %all-to-all-start = ((bf16[128,64,256]{2,1,0:T(8,128)(2,1)}), bf16[128,64,256]{2,1,0:T(8,128)(2,1)}, u32[]{:S(2)}, u32[]{:S(2)}) async-start(bf16[128,64,256]{2,1,0:T(8,128)(2,1)} %divide_convert_fusion), calls=%async_computation | async-start | bytes 8388608 | tf_op jit(solution)/shard_map/all_to_all | solution.py:15
  57.7 0.1 copy.35
  57.7 0.1 reshape.125
  57.9 0.1 copy.37
  57.9 0.7 copy.38
  58.6 50.2 %all-to-all-done = bf16[128,64,256]{2,1,0:T(8,128)(2,1)} async-done(((bf16[128,64,256]{2,1,0:T(8,128)(2,1)}), bf16[128,64,256]{2,1,0:T(8,128)(2,1)}, u32[]{:S(2)}, u32[]{:S(2)}) %all-to-all-start) | async-done | bytes 4194336 | tf_op jit(solution)/shard_map/all_to_all | solution.py:15
  108.9 6.9 %reshape_reshape.4 = bf16[16,8,64,1,2,128]{5,4,2,1,0,3:T(2,128)(2,1)} reshape(bf16[128,64,256]{2,1,0:T(8,128)(2,1)} %all-to-all-done) | data formatting | bytes 8388608 | tf_op jit(solution)/shard_map/reshape;reshape | solution.py:36
  115.8 10.8 %copy.32 = bf16[16,1,64,2,8,128]{5,4,3,2,0,1:T(8,128)(2,1)} copy(bf16[16,1,64,2,8,128]{5,3,2,4,0,1:T(2,128)(2,1)} %bitcast.21) | data formatting | bytes 8388608 | tf_op jit(solution)/shard_map/transpose | solution.py:37
  126.5 7.3 %reshape.121 = bf16[16,64,2048]{2,1,0:T(8,128)(2,1)} reshape(bf16[16,1,64,2,8,128]{5,4,3,2,0,1:T(8,128)(2,1)} %copy.32) | data formatting | bytes 8388608 | tf_op jit(solution)/shard_map/reshape | solution.py:38
  (5 shorter events, 0.0 us)
Async XLA Ops:
  6.4 2.0 %copy-start = (bf16[1,8192,256]{2,1,0:T(8,128)(2,1)}, bf16[1,8192,256]{2,1,0:T(8,128)(2,1)S(1)}, u32[]{:S(2)}) copy-start(bf16[1,8192,256]{2,1,0:T(8,128)(2,1)S(1)} %multiply_convert_fusion) | copy-start | bytes 12582916
  29.6 20.8 %all-to-all-start.1 = ((bf16[128,4,2]{1,2,0:T(2,128)(2,1)}), bf16[128,4,2]{1,2,0:T(2,128)(2,1)S(1)}, u32[]{:S(2)}, u32[]{:S(2)}) async-start(bf16[128,4,2]{1,2,0:T(2,128)(2,1)} %bitcast.3), calls=%async_computation.1 | async-start | bytes 131072 | tf_op jit(solution)/shard_map/all_to_all | solution.py:22
  50.5 58.4 %all-to-all-start = ((bf16[128,64,256]{2,1,0:T(8,128)(2,1)}), bf16[128,64,256]{2,1,0:T(8,128)(2,1)}, u32[]{:S(2)}, u32[]{:S(2)}) async-start(bf16[128,64,256]{2,1,0:T(8,128)(2,1)} %divide_convert_fusion), calls=%async_computation | async-start | bytes 8388608 | tf_op jit(solution)/shard_map/all_to_all | solution.py:15
where the time goes:
time: 135 us; the launch traced here: 134 us
  waiting for transfers between devices  53.3 us (39%)
  local copies, waits for them, and re-layouts  39.7 us (29%)
  other arithmetic  21.4 us (16%)
  starting transfers between devices  18.6 us (14%)
    all_to_all x1, waiting for transfers between devices, route(): lax.all_to_all(main_part.reshape((lead_count,) + main_part.shape[2:]), ('...  50.2 us
    all_to_all x1, starting transfers between devices, route(): lax.all_to_all(side_part.reshape((lead_count,) + side_part.shape[2:]), ('...  11.5 us
    transpose x1, local copies, waits for them, and re-layouts, regroup(): ordered = parted.transpose(0, 3, 2, 4, 1, 5)  10.8 us
    abs x1, local copies, waits for them, and re-layouts, on_device(): jnp.abs(blocks)  10.8 us
    reshape x1, local copies, waits for them, and re-layouts, regroup(): ordered.reshape(sections_count * layers_here, row_count, 2 * ranks_count...  7.27 us
    all_to_all x1, starting transfers between devices, route(): lax.all_to_all(main_part.reshape((lead_count,) + main_part.shape[2:]), ('...  7.15 us
    another operation x1, local copies, waits for them, and re-layouts, regroup(): arrived.reshape(sections_count, ranks_count, row_count, layers_here, 2, h...  6.89 us
    convert_element_type x1, other arithmetic, on_device(): scaled_here = (blocks / local_scale[:, :, None, :, None]).astype(jnp.bflo...  6.01 us
  transfers between devices with their start and end apart: 2, of which 2 were waited for; matrix products, arithmetic and copies ran while one was open for 5% of the time, Pallas kernels for 0%

commit v1 on v0

v1 whole, which is shorter than its diff:
```python
import functools

import jax
import jax.numpy as jnp
from jax import lax
from jax.experimental import pallas as pl
from jax.experimental.pallas import tpu as pltpu
from jax.sharding import PartitionSpec as P

BLOCK = 128
SCALE_FLOOR = 0.00390625
MESH = pl.DeviceIdType.MESH


def exchange(
    sections, ranks, k_ref, v_ref, g_ref, out_ref, scale_ref,
    raw, gain, scaled, rows_out, rows_in,
    load_sem, gain_sem, send_sem, recv_sem, row_send_sem, row_recv_sem,
):
    devices = sections * ranks
    section, rank = lax.axis_index("section"), lax.axis_index("tensor")
    me = section * ranks + rank
    model_rows = k_ref.shape[1]
    part = model_rows // sections
    share = part // ranks
    blocks = part // BLOCK

    def section_at(step):
        across, low, core = step // 4, step // 2 % 2, step % 2
        shift = jnp.where(across == 0, 1, jnp.where(across == 1, 3, jnp.where(across == 2, 2, 0)))
        my_low, my_x, my_core = section // 8, section // 2 % 4, section % 2
        return (my_low + low) % 2 * 8 + (my_x + shift) % 4 * 2 + (my_core + core) % 2

    def loads(step):
        rows = pl.ds(pl.multiple_of(section_at(step) * part, part), part)
        return [
            pltpu.make_async_copy(ref.at[0, rows], raw.at[kind, rows], load_sem.at[step, kind])
            for kind, ref in enumerate((k_ref, v_ref))
        ]

    pltpu.make_async_copy(g_ref, gain, gain_sem).start()

    @pl.loop(0, sections)
    def _(step):
        for copy in loads(step):
            copy.start()

    barrier = pltpu.get_barrier_semaphore()

    @pl.loop(1, devices)
    def _(step):
        peer = lax.rem(me + step, devices)
        pl.semaphore_signal(
            barrier, inc=1, device_id=(peer // ranks, peer % ranks), device_id_type=MESH
        )

    pltpu.make_async_copy(g_ref, gain, gain_sem).wait()
    lanes = lax.broadcasted_iota(jnp.int32, (1, BLOCK), 1)

    def prepare(step):
        target = section_at(step)
        for copy in loads(step):
            copy.wait()
        row_values = jnp.zeros((1, BLOCK), jnp.float32)
        for block in range(blocks):
            start = pl.multiple_of(target * part + block * BLOCK, BLOCK)
            rows = pl.ds(start, BLOCK)
            gain_rows = jnp.broadcast_to(gain[:, rows].astype(jnp.float32), (BLOCK, BLOCK)).T
            for kind in range(2):
                folded = (gain_rows * raw[kind, rows, :].astype(jnp.float32)).astype(jnp.bfloat16)
                folded = folded.astype(jnp.float32)
                peak = jnp.max(jnp.abs(folded), axis=(0, 1), keepdims=True)
                peak = jnp.maximum(peak, SCALE_FLOOR)
                scaled[kind, rows, :] = (folded * (1.0 / peak)).astype(jnp.bfloat16)
                lane = (block * 2 + kind) * ranks + rank
                row_values = jnp.where(lanes == lane, peak, row_values)
        rows_out[target] = row_values
        return target

    def send(target, other):
        peer = target * ranks + other
        rows = pl.ds(pl.multiple_of(peer * share, share), share)
        columns = pl.ds(pl.multiple_of(rank * BLOCK, BLOCK), BLOCK)

        @pl.when(peer != me)
        def _():
            pltpu.make_async_remote_copy(
                src_ref=rows_out.at[target],
                dst_ref=rows_in.at[me],
                send_sem=row_send_sem,
                recv_sem=row_recv_sem,
                device_id=(target, other),
                device_id_type=MESH,
            ).start()
            pltpu.make_async_remote_copy(
                src_ref=scaled.at[:, rows],
                dst_ref=out_ref.at[section, :, :, columns],
                send_sem=send_sem,
                recv_sem=recv_sem.at[section],
                device_id=(target, other),
                device_id_type=MESH,
            ).start()

    first = prepare(0)
    pl.semaphore_wait(barrier, devices - 1)

    def send_all(target):
        @pl.loop(0, ranks)
        def _(step):
            send(target, lax.rem(rank + step + 1, ranks))

    send_all(first)

    @pl.loop(1, sections)
    def _(step):
        send_all(prepare(step))

    mine = pl.ds(pl.multiple_of(me * share, share), share)
    columns = pl.ds(pl.multiple_of(rank * BLOCK, BLOCK), BLOCK)
    out_ref[section, :, :, columns] = scaled[:, mine, :]
    rows_in[me] = rows_out[section]

    some_rows = rows_in.at[pl.ds(0, devices - 1)]
    pltpu.make_async_copy(some_rows, some_rows, row_recv_sem).wait()
    peaks = jnp.max(rows_in[...].reshape(sections, ranks, 1, BLOCK), axis=1)
    width = 2 * ranks
    for block in range(blocks):
        for layer in range(sections):
            scale_ref[layer, block : block + 1, :] = peaks[layer, :, block * width : (block + 1) * width]

    for layer in range(sections):

        @pl.when(layer != section)
        def _():
            whole = out_ref.at[layer]
            pltpu.make_async_copy(whole, whole, recv_sem.at[layer]).wait()

        @pl.when(layer == section)
        def _():
            most = out_ref.at[layer, :, :, pl.ds(0, (ranks - 1) * BLOCK)]
            pltpu.make_async_copy(most, most, recv_sem.at[layer]).wait()

    pltpu.make_async_copy(some_rows, some_rows, row_send_sem).wait()
    sent = scaled.at[:, pl.ds(0, (devices - 1) * share)]
    pltpu.make_async_copy(sent, sent, send_sem).wait()


def settle(wide_ref, narrow_ref, scaled_ref, scale_ref, sem, scale_sem):
    layers, kinds, _, columns = wide_ref.shape
    copies = [
        pltpu.make_async_copy(
            wide_ref.at[layer, kind],
            scaled_ref.at[layer, :, pl.ds(kind * columns, columns)],
            sem.at[layer, kind],
        )
        for layer in range(layers)
        for kind in range(kinds)
    ]
    copies.append(pltpu.make_async_copy(narrow_ref, scale_ref, scale_sem))
    for copy in copies:
        copy.start()
    for copy in copies:
        copy.wait()


def on_device(key_weight, value_weight, norm_gain):
    sections, ranks = lax.axis_size("section"), lax.axis_size("tensor")
    devices = sections * ranks
    model_rows = key_weight.shape[1]
    share = model_rows // devices
    blocks = model_rows // sections // BLOCK
    anywhere = pl.BlockSpec(memory_space=pl.ANY)
    in_vmem = pl.BlockSpec(memory_space=pltpu.VMEM)
    wide, narrow = pl.pallas_call(
        functools.partial(exchange, sections, ranks),
        out_shape=(
            pltpu.VMEM((sections, 2, share, ranks * BLOCK), jnp.bfloat16),
            pltpu.VMEM((sections, blocks, 2 * ranks), jnp.float32),
        ),
        in_specs=[anywhere] * 3,
        out_specs=(in_vmem, in_vmem),
        scratch_shapes=[
            pltpu.VMEM((2, model_rows, BLOCK), jnp.bfloat16),
            pltpu.VMEM((1, model_rows), jnp.bfloat16),
            pltpu.VMEM((2, model_rows, BLOCK), jnp.bfloat16),
            pltpu.VMEM((sections, 1, BLOCK), jnp.float32),
            pltpu.VMEM((devices, 1, BLOCK), jnp.float32),
            pltpu.SemaphoreType.DMA((sections, 2)),
            pltpu.SemaphoreType.DMA,
            pltpu.SemaphoreType.DMA,
            pltpu.SemaphoreType.DMA((sections,)),
            pltpu.SemaphoreType.DMA,
            pltpu.SemaphoreType.DMA,
        ],
        compiler_params=pltpu.CompilerParams(
            collective_id=0, has_side_effects=True, vmem_limit_bytes=32 * 1024 * 1024
        ),
    )(key_weight, value_weight, norm_gain)
    return pl.pallas_call(
        settle,
        out_shape=(
            jax.ShapeDtypeStruct((sections, share, 2 * ranks * BLOCK), jnp.bfloat16),
            jax.ShapeDtypeStruct(narrow.shape, jnp.float32),
        ),
        in_specs=[in_vmem, in_vmem],
        out_specs=(anywhere, anywhere),
        scratch_shapes=[
            pltpu.SemaphoreType.DMA((sections, 2)),
            pltpu.SemaphoreType.DMA,
        ],
    )(wide, narrow)


def solution(mesh):
    placed = (P("section", None, "tensor"), P("section", None, "tensor"), P("section", None))
    return jax.shard_map(
        on_device,
        mesh=mesh,
        in_specs=placed,
        out_specs=(P(None, ("section", "tensor"), None), P(None, "section", None)),
        check_vma=False,
    )
```

time: 135 us -> 84.9 us (0.63)
  the two profiles are of different devices: /device:TPU:1 before, /device:TPU:11 now
where the time goes in v1:
time: 84.9 us; the launch traced here: 84.6 us
  Pallas kernels  77.5 us (91%)
  local copies, waits for them, and re-layouts  6.45 us (8%)
    pallas_call x1, Pallas kernels, on_device(): pl.pallas_call(functools.partial(exchange, sections, ranks), out_shape=(p...  73 us
    unnamed x10, local copies, waits for them, and re-layouts  6.45 us
    pallas_call x1, Pallas kernels, on_device(): pl.pallas_call(settle, out_shape=(jax.ShapeDtypeStruct((sections, share,...  4.46 us

profile of v1, /device:TPU:11, one launch (start us, length us, event | category | flops | bytes accessed | tf_op | source)
XLA Modules:
  0.0 84.6 jit_solution(3930461109001876429)
XLA Ops:
  0.6 0.0 copy-start.1
  0.6 1.6 %copy-done.1 = bf16[1,8192,128]{2,1,0:T(8,128)(2,1)S(1)} copy-done((bf16[1,8192,128]{2,1,0:T(8,128)(2,1)S(1)}, bf16[1,8192,128]{2,1,0:T(8,128)(2,1)}, u32[]{:S(2)}) %copy-start.1) | copy-done | bytes 2097176
  2.2 0.0 copy-start.2
  2.2 1.6 %copy-done.2 = bf16[1,8192,128]{2,1,0:T(8,128)(2,1)S(1)} copy-done((bf16[1,8192,128]{2,1,0:T(8,128)(2,1)S(1)}, bf16[1,8192,128]{2,1,0:T(8,128)(2,1)}, u32[]{:S(2)}) %copy-start.2) | copy-done | bytes 2097176
  3.8 0.0 copy-start.3
  3.8 0.8 copy-done.3
  4.6 73.0 %shard_map.50 = (bf16[16,2,64,1024]{3,2,1,0:T(8,128)(2,1)S(1)}, f32[16,4,16]{2,1,0:T(4,128)S(1)}) custom-call(bf16[1,8192,128]{2,1,0:T(8,128)(2,1)S(1)} %copy-done.1, bf16[1,8192,128]{2,1,0:T(8,128)(2,1)S(1)} %copy-done.2, bf16[1,8192]{1,0:T(2,128)(2,1)S(1)} %copy-done.3), custom_call_target="tpu_custom_call" | custom-call | tf_op jit(solution)/shard_map/pallas_call | solution.py:174
  77.6 0.0 copy-start
  77.6 1.9 %copy-done = bf16[16,2,64,1024]{3,2,1,0:T(8,128)(2,1)} copy-done((bf16[16,2,64,1024]{3,2,1,0:T(8,128)(2,1)}, bf16[16,2,64,1024]{3,2,1,0:T(8,128)(2,1)S(1)}, u32[]{:S(2)}) %copy-start) | copy-done | bytes 4194328
  79.5 0.0 copy-start.4
  79.6 0.6 copy-done.4
  80.1 4.5 %shard_map.51 = (bf16[16,64,2048]{2,1,0:T(8,128)(2,1)}, f32[16,4,16]{2,1,0:T(4,128)}) custom-call(bf16[16,2,64,1024]{3,2,1,0:T(8,128)(2,1)} %copy-done, f32[16,4,16]{2,1,0:T(4,128)} %copy-done.4), custom_call_target="tpu_custom_call" | custom-call | tf_op jit(solution)/shard_map/pallas_call | solution.py:199
Async XLA Ops:
  0.6 1.6 %copy-start.1 = (bf16[1,8192,128]{2,1,0:T(8,128)(2,1)S(1)}, bf16[1,8192,128]{2,1,0:T(8,128)(2,1)}, u32[]{:S(2)}) copy-start(bf16[1,8192,128]{2,1,0:T(8,128)(2,1)} %k_ref.1) | copy-start | bytes 6291460
  2.2 1.6 %copy-start.2 = (bf16[1,8192,128]{2,1,0:T(8,128)(2,1)S(1)}, bf16[1,8192,128]{2,1,0:T(8,128)(2,1)}, u32[]{:S(2)}) copy-start(bf16[1,8192,128]{2,1,0:T(8,128)(2,1)} %v_ref.1) | copy-start | bytes 6291460
  3.8 0.8 copy-start.3
  77.6 1.9 %copy-start = (bf16[16,2,64,1024]{3,2,1,0:T(8,128)(2,1)}, bf16[16,2,64,1024]{3,2,1,0:T(8,128)(2,1)S(1)}, u32[]{:S(2)}) copy-start(bf16[16,2,64,1024]{3,2,1,0:T(8,128)(2,1)S(1)} %get-tuple-element.4.wide_ref) | copy-start | bytes 12582916
  79.5 0.6 copy-start.4

commit v2 on v1

--- a/solution.py
+++ b/solution.py
@@ -171,6 +171,7 @@
     blocks = model_rows // sections // BLOCK
     anywhere = pl.BlockSpec(memory_space=pl.ANY)
     in_vmem = pl.BlockSpec(memory_space=pltpu.VMEM)
+    in_space = pltpu.with_memory_space_constraint
     wide, narrow = pl.pallas_call(
         functools.partial(exchange, sections, ranks),
         out_shape=(
@@ -195,7 +196,7 @@
         compiler_params=pltpu.CompilerParams(
             collective_id=0, has_side_effects=True, vmem_limit_bytes=32 * 1024 * 1024
         ),
-    )(key_weight, value_weight, norm_gain)
+    )(*(in_space(array, pltpu.HBM) for array in (key_weight, value_weight, norm_gain)))
     return pl.pallas_call(
         settle,
         out_shape=(
@@ -208,7 +209,8 @@
             pltpu.SemaphoreType.DMA((sections, 2)),
             pltpu.SemaphoreType.DMA,
         ],
-    )(wide, narrow)
+        compiler_params=pltpu.CompilerParams(vmem_limit_bytes=4 * 1024 * 1024),
+    )(in_space(wide, pltpu.VMEM), in_space(narrow, pltpu.VMEM))
 
 
 def solution(mesh):

time: 84.9 us -> 70.7 us (0.83)
  Pallas kernels: 77.5 us -> 70 us
  local copies, waits for them, and re-layouts: 6.45 us -> 0 us
    unnamed x10 -> x0, local copies, waits for them, and re-layouts: 6.45 us -> none
    pallas_call x1, Pallas kernels: 73 us -> 67.7 us  [on_device(): pl.pallas_call(functools.partial(exchange, sections, ranks), out_shape=(p...]
    pallas_call x1, Pallas kernels: 4.46 us -> 2.28 us  [on_device(): pl.pallas_call(settle, out_shape=(jax.ShapeDtypeStruct((sections, share,...]
where the time goes in v2:
time: 70.7 us; the launch traced here: 70.6 us
  Pallas kernels  70 us (99%)
    pallas_call x1, Pallas kernels, on_device(): pl.pallas_call(functools.partial(exchange, sections, ranks), out_shape=(p...  67.7 us
    pallas_call x1, Pallas kernels, on_device(): pl.pallas_call(settle, out_shape=(jax.ShapeDtypeStruct((sections, share,...  2.28 us

profile of v2, /device:TPU:11, one launch (start us, length us, event | category | flops | bytes accessed | tf_op | source)
XLA Modules:
  0.0 70.6 jit_solution(1290539297906292293)
XLA Ops:
  0.6 67.7 %shard_map.50 = (bf16[16,2,64,1024]{3,2,1,0:T(8,128)(2,1)S(1)}, f32[16,4,16]{2,1,0:T(4,128)S(1)}) custom-call(bf16[1,8192,128]{2,1,0:T(8,128)(2,1)} %k_ref.1, bf16[1,8192,128]{2,1,0:T(8,128)(2,1)} %v_ref.1, bf16[1,8192]{1,0:T(2,128)(2,1)} %g_ref.1), custom_call_target="tpu_custom_call" | custom-call | tf_op jit(solution)/shard_map/pallas_call | solution.py:175
  68.4 2.3 %shard_map.51 = (bf16[16,64,2048]{2,1,0:T(8,128)(2,1)}, f32[16,4,16]{2,1,0:T(4,128)}) custom-call(bf16[16,2,64,1024]{3,2,1,0:T(8,128)(2,1)S(1)} %get-tuple-element.4.wide_ref, f32[16,4,16]{2,1,0:T(4,128)S(1)} %get-tuple-element.5.narrow_ref), custom_call_target="tpu_custom_call" | custom-call | tf_op jit(solution)/shard_map/pallas_call | solution.py:200

commit v3 on v2

v3 whole, which is shorter than its diff:
```python
import functools
import itertools

import jax
import jax.numpy as jnp
from jax import lax
from jax.experimental import pallas as pl
from jax.experimental.pallas import tpu as pltpu
from jax.sharding import PartitionSpec as P

BLOCK = 128
SCALE_FLOOR = 0.00390625
MESH = pl.DeviceIdType.MESH
SIDE = 4
CHUNK = 4
AHEAD = 3


def hops(offset):
    return sum(min(value, SIDE - value) for value in offset[:3])


def axes_used(offset):
    return sum(value != 0 for value in offset[:3])


def send_order():
    chips = list(itertools.product(range(SIDE), repeat=3))
    kind = {chip: tuple(sorted(min(v, SIDE - v) for v in chip)) for chip in chips}
    order = []
    for alike in sorted(set(kind.values()), key=lambda k: (-sum(k), k)):
        turn = []
        for chip in chips:
            if kind[chip] != alike:
                continue
            for shift in range(3):
                rolled = chip[-shift:] + chip[:-shift] if shift else chip
                for member in (rolled, tuple(-v % SIDE for v in rolled)):
                    if member not in turn:
                        turn.append(member)
        order += [member + (core,) for core in range(2) for member in turn]
    order.remove((0, 0, 0, 0))
    return order


ORDER = send_order()
LINES = [o for o in ORDER if axes_used(o) <= 1]
PLANES = [o for o in ORDER if axes_used(o) == 2]
REST = [o for o in ORDER if axes_used(o) == 3]


def block_of(offset):
    return offset[:2] + (offset[2] // 2, offset[3])


BLOCKS = list(dict.fromkeys(block_of(o) for o in LINES + PLANES + REST))
CHUNKS = [BLOCKS[i : i + CHUNK] for i in range(0, len(BLOCKS), CHUNK)]
PLACE = {block: (i // CHUNK, i % CHUNK) for i, block in enumerate(BLOCKS)}


def exchange(
    sections, ranks, k_ref, v_ref, g_ref, out_ref, scale_ref,
    raw, gain, scaled, rows_out, rows_in,
    load_sem, gain_sem, send_sem, recv_sem, row_send_sem, row_recv_sem, plane_sem, rest_sem,
):
    devices = sections * ranks
    section, rank = lax.axis_index("section"), lax.axis_index("tensor")
    me = section * ranks + rank
    model_rows = k_ref.shape[1]
    part = model_rows // sections
    share = part // ranks
    blocks = part // BLOCK
    core, my_x = section % 2, section // 2 % SIDE
    my_y, my_z = rank // SIDE * 2 + section // (2 * SIDE), rank % SIDE
    toward = 1 - 2 * (my_z % 2)

    def target(offset):
        x, y = (my_x + offset[0]) % SIDE, (my_y + offset[1]) % SIDE
        z = (my_z + toward * offset[2] + SIDE) % SIDE
        return (y % 2 * SIDE + x) * 2 + (core + offset[3]) % 2, y // 2 * SIDE + z

    def block_at(block):
        there, other = target(block[:2] + (block[2] * 2, block[3]))
        return there, other // 2

    def load(chunk):
        for place, block in enumerate(CHUNKS[chunk]):
            there, inner = block_at(block)
            rows = pl.ds(pl.multiple_of(there * part + inner * BLOCK, BLOCK), BLOCK)
            for kind, ref in enumerate((k_ref, v_ref)):
                pltpu.make_async_copy(
                    ref.at[0, rows], raw.at[chunk, kind, place], load_sem.at[chunk]
                ).start()

    lanes = lax.broadcasted_iota(jnp.int32, (1, BLOCK), 1)

    def compute(chunk):
        if chunk + AHEAD < len(CHUNKS):
            load(chunk + AHEAD)
        pltpu.make_async_copy(raw.at[chunk], raw.at[chunk], load_sem.at[chunk]).wait()
        for place, block in enumerate(CHUNKS[chunk]):
            there, inner = block_at(block)
            start = pl.multiple_of(there * part + inner * BLOCK, BLOCK)
            gain_rows = gain[:, pl.ds(start, BLOCK)].astype(jnp.float32)
            gain_rows = jnp.broadcast_to(gain_rows, (BLOCK, BLOCK)).T
            row_values = rows_out[there]
            for kind in range(2):
                folded = gain_rows * raw[chunk, kind, place].astype(jnp.float32)
                folded = folded.astype(jnp.bfloat16).astype(jnp.float32)
                peak = jnp.max(jnp.abs(folded), axis=(0, 1), keepdims=True)
                peak = jnp.maximum(peak, SCALE_FLOOR)
                scaled[chunk, place, kind] = (folded * (1.0 / peak)).astype(jnp.bfloat16)
                lane = (inner * 2 + kind) * ranks + rank
                row_values = jnp.where(lanes == lane, peak, row_values)
            rows_out[there] = row_values

    columns = pl.ds(pl.multiple_of(rank * BLOCK, BLOCK), BLOCK)

    def piece(offset):
        there, other = target(offset)
        chunk, place = PLACE[block_of(offset)]
        half = pl.multiple_of(other % 2 * share, share)
        return there, other, scaled.at[chunk, place, :, pl.ds(half, share)]

    def send(offset):
        there, other, source = piece(offset)
        pltpu.make_async_remote_copy(
            src_ref=source,
            dst_ref=out_ref.at[section, :, :, columns],
            send_sem=send_sem,
            recv_sem=recv_sem.at[section],
            device_id=(there, other),
            device_id_type=MESH,
        ).start()

    def greet(semaphore):
        for offset in LINES:
            pl.semaphore_signal(
                semaphore, inc=1, device_id=target(offset), device_id_type=MESH
            )

    done = 0

    def send_group(group, done):
        for offset in group:
            while PLACE[block_of(offset)][0] >= done:
                compute(done)
                done += 1
            send(offset)
        return done

    barrier = pltpu.get_barrier_semaphore()
    gain_copy = pltpu.make_async_copy(g_ref, gain, gain_sem)
    gain_copy.start()
    load(0)
    greet(barrier)
    for chunk in range(1, AHEAD):
        load(chunk)
    rows_out[...] = jnp.zeros_like(rows_out)
    gain_copy.wait()
    compute(0)
    done = 1
    pl.semaphore_wait(barrier, len(LINES))
    greet(plane_sem)
    done = send_group(LINES, done)
    pl.semaphore_wait(plane_sem, len(LINES))
    greet(rest_sem)
    done = send_group(PLANES, done)
    while done < len(CHUNKS):
        compute(done)
        done += 1
    pl.semaphore_wait(rest_sem, len(LINES))

    @pl.loop(1, devices)
    def _(step):
        peer = lax.rem(me + step, devices)
        there, other = peer // ranks, peer % ranks
        pltpu.make_async_remote_copy(
            src_ref=rows_out.at[there],
            dst_ref=rows_in.at[me],
            send_sem=row_send_sem,
            recv_sem=row_recv_sem,
            device_id=(there, other),
            device_id_type=MESH,
        ).start()

    send_group(REST, done)

    out_ref[section, :, :, columns] = piece((0, 0, 0, 0))[2][...]
    rows_in[me] = rows_out[section]

    some_rows = rows_in.at[pl.ds(0, devices - 1)]
    pltpu.make_async_copy(some_rows, some_rows, row_recv_sem).wait()
    peaks = jnp.max(rows_in[...].reshape(sections, ranks, 1, BLOCK), axis=1)
    width = 2 * ranks
    for block in range(blocks):
        for layer in range(sections):
            scale_ref[layer, block : block + 1, :] = peaks[layer, :, block * width : (block + 1) * width]

    for layer in range(sections):

        @pl.when(layer != section)
        def _():
            whole = out_ref.at[layer]
            pltpu.make_async_copy(whole, whole, recv_sem.at[layer]).wait()

        @pl.when(layer == section)
        def _():
            most = out_ref.at[layer, :, :, pl.ds(0, (ranks - 1) * BLOCK)]
            pltpu.make_async_copy(most, most, recv_sem.at[layer]).wait()

    pltpu.make_async_copy(some_rows, some_rows, row_send_sem).wait()
    half = scaled.at[0, 0, :, pl.ds(0, share)]
    all_but_one = scaled.at[pl.ds(0, len(CHUNKS) - 1)]
    pltpu.make_async_copy(all_but_one, all_but_one, send_sem).wait()
    last = scaled.at[0, pl.ds(0, CHUNK - 1)]
    pltpu.make_async_copy(last, last, send_sem).wait()
    pltpu.make_async_copy(half, half, send_sem).wait()


def settle(wide_ref, narrow_ref, scaled_ref, scale_ref, sem, scale_sem):
    layers, kinds, _, columns = wide_ref.shape
    copies = [
        pltpu.make_async_copy(
            wide_ref.at[layer, kind],
            scaled_ref.at[layer, :, pl.ds(kind * columns, columns)],
            sem.at[layer, kind],
        )
        for layer in range(layers)
        for kind in range(kinds)
    ]
    copies.append(pltpu.make_async_copy(narrow_ref, scale_ref, scale_sem))
    for copy in copies:
        copy.start()
    for copy in copies:
        copy.wait()


def on_device(key_weight, value_weight, norm_gain):
    sections, ranks = lax.axis_size("section"), lax.axis_size("tensor")
    devices = sections * ranks
    model_rows = key_weight.shape[1]
    share = model_rows // devices
    blocks = model_rows // sections // BLOCK
    anywhere = pl.BlockSpec(memory_space=pl.ANY)
    in_vmem = pl.BlockSpec(memory_space=pltpu.VMEM)
    in_space = pltpu.with_memory_space_constraint
    wide, narrow = pl.pallas_call(
        functools.partial(exchange, sections, ranks),
        out_shape=(
            pltpu.VMEM((sections, 2, share, ranks * BLOCK), jnp.bfloat16),
            pltpu.VMEM((sections, blocks, 2 * ranks), jnp.float32),
        ),
        in_specs=[anywhere] * 3,
        out_specs=(in_vmem, in_vmem),
        scratch_shapes=[
            pltpu.VMEM((len(CHUNKS), 2, CHUNK, BLOCK, BLOCK), jnp.bfloat16),
            pltpu.VMEM((1, model_rows), jnp.bfloat16),
            pltpu.VMEM((len(CHUNKS), CHUNK, 2, BLOCK, BLOCK), jnp.bfloat16),
            pltpu.VMEM((sections, 1, BLOCK), jnp.float32),
            pltpu.VMEM((devices, 1, BLOCK), jnp.float32),
            pltpu.SemaphoreType.DMA((len(CHUNKS),)),
            pltpu.SemaphoreType.DMA,
            pltpu.SemaphoreType.DMA,
            pltpu.SemaphoreType.DMA((sections,)),
            pltpu.SemaphoreType.DMA,
            pltpu.SemaphoreType.DMA,
            pltpu.SemaphoreType.REGULAR,
            pltpu.SemaphoreType.REGULAR,
        ],
        compiler_params=pltpu.CompilerParams(
            collective_id=0, has_side_effects=True, vmem_limit_bytes=32 * 1024 * 1024
        ),
    )(*(in_space(array, pltpu.HBM) for array in (key_weight, value_weight, norm_gain)))
    return pl.pallas_call(
        settle,
        out_shape=(
            jax.ShapeDtypeStruct((sections, share, 2 * ranks * BLOCK), jnp.bfloat16),
            jax.ShapeDtypeStruct(narrow.shape, jnp.float32),
        ),
        in_specs=[in_vmem, in_vmem],
        out_specs=(anywhere, anywhere),
        scratch_shapes=[
            pltpu.SemaphoreType.DMA((sections, 2)),
            pltpu.SemaphoreType.DMA,
        ],
        compiler_params=pltpu.CompilerParams(vmem_limit_bytes=4 * 1024 * 1024),
    )(in_space(wide, pltpu.VMEM), in_space(narrow, pltpu.VMEM))


def solution(mesh):
    placed = (P("section", None, "tensor"), P("section", None, "tensor"), P("section", None))
    return jax.shard_map(
        on_device,
        mesh=mesh,
        in_specs=placed,
        out_specs=(P(None, ("section", "tensor"), None), P(None, "section", None)),
        check_vma=False,
    )
```

time: 70.7 us -> 62.5 us (0.88)
  the two profiles are of different devices: /device:TPU:11 before, /device:TPU:1 now
where the time goes in v3:
time: 62.5 us; the launch traced here: 62.3 us
  Pallas kernels  61.6 us (99%)
  between operations  0.64 us (1%)
    pallas_call x1, Pallas kernels, on_device(): pl.pallas_call(functools.partial(exchange, sections, ranks), out_shape=(p...  59.4 us
    pallas_call x1, Pallas kernels, on_device(): pl.pallas_call(settle, out_shape=(jax.ShapeDtypeStruct((sections, share,...  2.28 us

profile of v3, /device:TPU:1, one launch (start us, length us, event | category | flops | bytes accessed | tf_op | source)
XLA Modules:
  0.0 62.3 jit_solution(345017170370475249)
XLA Ops:
  0.6 59.4 %shard_map.50 = (bf16[16,2,64,1024]{3,2,1,0:T(8,128)(2,1)S(1)}, f32[16,4,16]{2,1,0:T(4,128)S(1)}) custom-call(bf16[1,8192,128]{2,1,0:T(8,128)(2,1)} %k_ref.1, bf16[1,8192,128]{2,1,0:T(8,128)(2,1)} %v_ref.1, bf16[1,8192]{1,0:T(2,128)(2,1)} %g_ref.1), custom_call_target="tpu_custom_call" | custom-call | tf_op jit(solution)/shard_map/pallas_call | solution.py:248
  60.0 2.3 %shard_map.51 = (bf16[16,64,2048]{2,1,0:T(8,128)(2,1)}, f32[16,4,16]{2,1,0:T(4,128)}) custom-call(bf16[16,2,64,1024]{3,2,1,0:T(8,128)(2,1)S(1)} %get-tuple-element.4.wide_ref, f32[16,4,16]{2,1,0:T(4,128)S(1)} %get-tuple-element.5.narrow_ref), custom_call_target="tpu_custom_call" | custom-call | tf_op jit(solution)/shard_map/pallas_call | solution.py:275

commit v4 on v3

--- a/solution.py
+++ b/solution.py
@@ -165,7 +165,7 @@
     done = send_group(LINES, done)
     pl.semaphore_wait(plane_sem, len(LINES))
     greet(rest_sem)
-    done = send_group(PLANES, done)
+    done = send_group(PLANES[:36], done)
     while done < len(CHUNKS):
         compute(done)
         done += 1
@@ -184,7 +184,7 @@
             device_id_type=MESH,
         ).start()
 
-    send_group(REST, done)
+    send_group(REST + PLANES[36:], done)
 
     out_ref[section, :, :, columns] = piece((0, 0, 0, 0))[2][...]
     rows_in[me] = rows_out[section]

time: 62.5 us -> 61.3 us (0.981)
  Pallas kernels: 61.6 us -> 60.5 us
    pallas_call x1, Pallas kernels: 59.4 us -> 58.2 us  [on_device(): pl.pallas_call(functools.partial(exchange, sections, ranks), out_shape=(p...]
where the time goes in v4:
time: 61.3 us; the launch traced here: 61.1 us
  Pallas kernels  60.5 us (99%)
  between operations  0.64 us (1%)
    pallas_call x1, Pallas kernels, on_device(): pl.pallas_call(functools.partial(exchange, sections, ranks), out_shape=(p...  58.2 us
    pallas_call x1, Pallas kernels, on_device(): pl.pallas_call(settle, out_shape=(jax.ShapeDtypeStruct((sections, share,...  2.28 us

profile of v4, /device:TPU:1, one launch (start us, length us, event | category | flops | bytes accessed | tf_op | source)
XLA Modules:
  0.0 61.1 jit_solution(7371176763513925645)
XLA Ops:
  0.6 58.2 %shard_map.50 = (bf16[16,2,64,1024]{3,2,1,0:T(8,128)(2,1)S(1)}, f32[16,4,16]{2,1,0:T(4,128)S(1)}) custom-call(bf16[1,8192,128]{2,1,0:T(8,128)(2,1)} %k_ref.1, bf16[1,8192,128]{2,1,0:T(8,128)(2,1)} %v_ref.1, bf16[1,8192]{1,0:T(2,128)(2,1)} %g_ref.1), custom_call_target="tpu_custom_call" | custom-call | tf_op jit(solution)/shard_map/pallas_call | solution.py:248
  58.8 2.3 %shard_map.51 = (bf16[16,64,2048]{2,1,0:T(8,128)(2,1)}, f32[16,4,16]{2,1,0:T(4,128)}) custom-call(bf16[16,2,64,1024]{3,2,1,0:T(8,128)(2,1)S(1)} %get-tuple-element.4.wide_ref, f32[16,4,16]{2,1,0:T(4,128)S(1)} %get-tuple-element.5.narrow_ref), custom_call_target="tpu_custom_call" | custom-call | tf_op jit(solution)/shard_map/pallas_call | solution.py:275

commit v5 on v4

--- a/solution.py
+++ b/solution.py
@@ -89,7 +89,7 @@
             rows = pl.ds(pl.multiple_of(there * part + inner * BLOCK, BLOCK), BLOCK)
             for kind, ref in enumerate((k_ref, v_ref)):
                 pltpu.make_async_copy(
-                    ref.at[0, rows], raw.at[chunk, kind, place], load_sem.at[chunk]
+                    ref.at[0, rows], raw.at[(chunk * 2 + kind) * CHUNK + place], load_sem.at[chunk]
                 ).start()
 
     lanes = lax.broadcasted_iota(jnp.int32, (1, BLOCK), 1)
@@ -97,7 +97,8 @@
     def compute(chunk):
         if chunk + AHEAD < len(CHUNKS):
             load(chunk + AHEAD)
-        pltpu.make_async_copy(raw.at[chunk], raw.at[chunk], load_sem.at[chunk]).wait()
+        here = raw.at[pl.ds(chunk * 2 * CHUNK, 2 * CHUNK)]
+        pltpu.make_async_copy(here, here, load_sem.at[chunk]).wait()
         for place, block in enumerate(CHUNKS[chunk]):
             there, inner = block_at(block)
             start = pl.multiple_of(there * part + inner * BLOCK, BLOCK)
@@ -105,7 +106,7 @@
             gain_rows = jnp.broadcast_to(gain_rows, (BLOCK, BLOCK)).T
             row_values = rows_out[there]
             for kind in range(2):
-                folded = gain_rows * raw[chunk, kind, place].astype(jnp.float32)
+                folded = gain_rows * raw[(chunk * 2 + kind) * CHUNK + place].astype(jnp.float32)
                 folded = folded.astype(jnp.bfloat16).astype(jnp.float32)
                 peak = jnp.max(jnp.abs(folded), axis=(0, 1), keepdims=True)
                 peak = jnp.maximum(peak, SCALE_FLOOR)
@@ -128,7 +129,7 @@
             src_ref=source,
             dst_ref=out_ref.at[section, :, :, columns],
             send_sem=send_sem,
-            recv_sem=recv_sem.at[section],
+            recv_sem=recv_sem,
             device_id=(there, other),
             device_id_type=MESH,
         ).start()
@@ -159,7 +160,8 @@
     rows_out[...] = jnp.zeros_like(rows_out)
     gain_copy.wait()
     compute(0)
-    done = 1
+    compute(1)
+    done = 2
     pl.semaphore_wait(barrier, len(LINES))
     greet(plane_sem)
     done = send_group(LINES, done)
@@ -197,25 +199,10 @@
         for layer in range(sections):
             scale_ref[layer, block : block + 1, :] = peaks[layer, :, block * width : (block + 1) * width]
 
-    for layer in range(sections):
-
-        @pl.when(layer != section)
-        def _():
-            whole = out_ref.at[layer]
-            pltpu.make_async_copy(whole, whole, recv_sem.at[layer]).wait()
-
-        @pl.when(layer == section)
-        def _():
-            most = out_ref.at[layer, :, :, pl.ds(0, (ranks - 1) * BLOCK)]
-            pltpu.make_async_copy(most, most, recv_sem.at[layer]).wait()
-
+    pieces = raw.at[pl.ds(0, devices - 1)]
+    pltpu.make_async_copy(pieces, pieces, recv_sem).wait()
     pltpu.make_async_copy(some_rows, some_rows, row_send_sem).wait()
-    half = scaled.at[0, 0, :, pl.ds(0, share)]
-    all_but_one = scaled.at[pl.ds(0, len(CHUNKS) - 1)]
-    pltpu.make_async_copy(all_but_one, all_but_one, send_sem).wait()
-    last = scaled.at[0, pl.ds(0, CHUNK - 1)]
-    pltpu.make_async_copy(last, last, send_sem).wait()
-    pltpu.make_async_copy(half, half, send_sem).wait()
+    pltpu.make_async_copy(pieces, pieces, send_sem).wait()
 
 
 def settle(wide_ref, narrow_ref, scaled_ref, scale_ref, sem, scale_sem):
@@ -254,7 +241,7 @@
         in_specs=[anywhere] * 3,
         out_specs=(in_vmem, in_vmem),
         scratch_shapes=[
-            pltpu.VMEM((len(CHUNKS), 2, CHUNK, BLOCK, BLOCK), jnp.bfloat16),
+            pltpu.VMEM((len(BLOCKS) * 2, BLOCK, BLOCK), jnp.bfloat16),
             pltpu.VMEM((1, model_rows), jnp.bfloat16),
             pltpu.VMEM((len(CHUNKS), CHUNK, 2, BLOCK, BLOCK), jnp.bfloat16),
             pltpu.VMEM((sections, 1, BLOCK), jnp.float32),
@@ -262,7 +249,7 @@
             pltpu.SemaphoreType.DMA((len(CHUNKS),)),
             pltpu.SemaphoreType.DMA,
             pltpu.SemaphoreType.DMA,
-            pltpu.SemaphoreType.DMA((sections,)),
+            pltpu.SemaphoreType.DMA,
             pltpu.SemaphoreType.DMA,
             pltpu.SemaphoreType.DMA,
             pltpu.SemaphoreType.REGULAR,

time: 61.3 us -> 61 us (level)
  no operation moved by 1% of the time
where the time goes in v5:
time: 61 us; the launch traced here: 60.8 us
  Pallas kernels  60.2 us (99%)
  between operations  0.64 us (1%)
    pallas_call x1, Pallas kernels, on_device(): pl.pallas_call(functools.partial(exchange, sections, ranks), out_shape=(p...  57.9 us
    pallas_call x1, Pallas kernels, on_device(): pl.pallas_call(settle, out_shape=(jax.ShapeDtypeStruct((sections, share,...  2.28 us

profile of v5, /device:TPU:1, one launch (start us, length us, event | category | flops | bytes accessed | tf_op | source)
XLA Modules:
  0.0 60.8 jit_solution(17304599928273504615)
XLA Ops:
  0.6 57.9 %shard_map.50 = (bf16[16,2,64,1024]{3,2,1,0:T(8,128)(2,1)S(1)}, f32[16,4,16]{2,1,0:T(4,128)S(1)}) custom-call(bf16[1,8192,128]{2,1,0:T(8,128)(2,1)} %k_ref.1, bf16[1,8192,128]{2,1,0:T(8,128)(2,1)} %v_ref.1, bf16[1,8192]{1,0:T(2,128)(2,1)} %g_ref.1), custom_call_target="tpu_custom_call" | custom-call | tf_op jit(solution)/shard_map/pallas_call | solution.py:235
  58.5 2.3 %shard_map.51 = (bf16[16,64,2048]{2,1,0:T(8,128)(2,1)}, f32[16,4,16]{2,1,0:T(4,128)}) custom-call(bf16[16,2,64,1024]{3,2,1,0:T(8,128)(2,1)S(1)} %get-tuple-element.4.wide_ref, f32[16,4,16]{2,1,0:T(4,128)S(1)} %get-tuple-element.5.narrow_ref), custom_call_target="tpu_custom_call" | custom-call | tf_op jit(solution)/shard_map/pallas_call | solution.py:262

commit v6 on v5

--- a/solution.py
+++ b/solution.py
@@ -60,7 +60,7 @@
 
 def exchange(
     sections, ranks, k_ref, v_ref, g_ref, out_ref, scale_ref,
-    raw, gain, scaled, rows_out, rows_in,
+    raw, gain, scaled, rows_out, rows_in, rows_at,
     load_sem, gain_sem, send_sem, recv_sem, row_send_sem, row_recv_sem, plane_sem, rest_sem,
 ):
     devices = sections * ranks
@@ -111,7 +111,7 @@
                 peak = jnp.max(jnp.abs(folded), axis=(0, 1), keepdims=True)
                 peak = jnp.maximum(peak, SCALE_FLOOR)
                 scaled[chunk, place, kind] = (folded * (1.0 / peak)).astype(jnp.bfloat16)
-                lane = (inner * 2 + kind) * ranks + rank
+                lane = (kind * sections + section) * blocks + inner
                 row_values = jnp.where(lanes == lane, peak, row_values)
             rows_out[there] = row_values
 
@@ -173,35 +173,47 @@
         done += 1
     pl.semaphore_wait(rest_sem, len(LINES))
 
-    @pl.loop(1, devices)
-    def _(step):
-        peer = lax.rem(me + step, devices)
-        there, other = peer // ranks, peer % ranks
+    def send_row(source, landing, there, other, stage):
         pltpu.make_async_remote_copy(
-            src_ref=rows_out.at[there],
-            dst_ref=rows_in.at[me],
-            send_sem=row_send_sem,
-            recv_sem=row_recv_sem,
+            src_ref=source,
+            dst_ref=landing,
+            send_sem=row_send_sem.at[stage],
+            recv_sem=row_recv_sem.at[stage],
             device_id=(there, other),
             device_id_type=MESH,
         ).start()
 
+    def wait_rows(semaphores, stage, count):
+        some = rows_in.at[pl.ds(0, count)]
+        pltpu.make_async_copy(some, some, semaphores.at[stage]).wait()
+
+    @pl.loop(1, sections)
+    def _(step):
+        there = lax.rem(section + step, sections)
+        send_row(rows_out.at[there], rows_in.at[section], there, rank, 0)
+
     send_group(REST + PLANES[36:], done)
-
+    rows_in[section] = rows_out[section]
+    wait_rows(row_recv_sem, 0, sections - 1)
+    rows_at[rank] = jnp.max(rows_in[...], axis=0)
     out_ref[section, :, :, columns] = piece((0, 0, 0, 0))[2][...]
-    rows_in[me] = rows_out[section]
-
-    some_rows = rows_in.at[pl.ds(0, devices - 1)]
-    pltpu.make_async_copy(some_rows, some_rows, row_recv_sem).wait()
-    peaks = jnp.max(rows_in[...].reshape(sections, ranks, 1, BLOCK), axis=1)
-    width = 2 * ranks
-    for block in range(blocks):
-        for layer in range(sections):
-            scale_ref[layer, block : block + 1, :] = peaks[layer, :, block * width : (block + 1) * width]
+
+    @pl.loop(1, ranks)
+    def _(step):
+        other = lax.rem(rank + step, ranks)
+        send_row(rows_at.at[rank], rows_at.at[rank], section, other, 1)
+
+    wait_rows(row_recv_sem, 1, ranks - 1)
+    by_rank = jnp.concatenate([rows_at[other] for other in range(ranks)] * (BLOCK // ranks), axis=0).T
+    first_half, second_half = by_rank[: BLOCK // 2], by_rank[BLOCK // 2 :]
+    all_scales = jnp.where(lanes < ranks, first_half, second_half)
+    for layer in range(sections):
+        scale_ref[layer] = all_scales[layer * blocks : (layer + 1) * blocks, : 2 * ranks]
 
     pieces = raw.at[pl.ds(0, devices - 1)]
     pltpu.make_async_copy(pieces, pieces, recv_sem).wait()
-    pltpu.make_async_copy(some_rows, some_rows, row_send_sem).wait()
+    wait_rows(row_send_sem, 0, sections - 1)
+    wait_rows(row_send_sem, 1, ranks - 1)
     pltpu.make_async_copy(pieces, pieces, send_sem).wait()
 
 
@@ -245,13 +257,14 @@
             pltpu.VMEM((1, model_rows), jnp.bfloat16),
             pltpu.VMEM((len(CHUNKS), CHUNK, 2, BLOCK, BLOCK), jnp.bfloat16),
             pltpu.VMEM((sections, 1, BLOCK), jnp.float32),
-            pltpu.VMEM((devices, 1, BLOCK), jnp.float32),
+            pltpu.VMEM((sections, 1, BLOCK), jnp.float32),
+            pltpu.VMEM((ranks, 1, BLOCK), jnp.float32),
             pltpu.SemaphoreType.DMA((len(CHUNKS),)),
             pltpu.SemaphoreType.DMA,
             pltpu.SemaphoreType.DMA,
             pltpu.SemaphoreType.DMA,
-            pltpu.SemaphoreType.DMA,
-            pltpu.SemaphoreType.DMA,
+            pltpu.SemaphoreType.DMA((2,)),
+            pltpu.SemaphoreType.DMA((2,)),
             pltpu.SemaphoreType.REGULAR,
             pltpu.SemaphoreType.REGULAR,
         ],

time: 61 us -> 60.7 us (level)
  no operation moved by 1% of the time
where the time goes in v6:
time: 60.7 us; the launch traced here: 60.5 us
  Pallas kernels  59.8 us (99%)
  between operations  0.64 us (1%)
    pallas_call x1, Pallas kernels, on_device(): pl.pallas_call(functools.partial(exchange, sections, ranks), out_shape=(p...  57.6 us
    pallas_call x1, Pallas kernels, on_device(): pl.pallas_call(settle, out_shape=(jax.ShapeDtypeStruct((sections, share,...  2.28 us

profile of v6, /device:TPU:1, one launch (start us, length us, event | category | flops | bytes accessed | tf_op | source)
XLA Modules:
  0.0 60.5 jit_solution(269412933929410774)
XLA Ops:
  0.6 57.6 %shard_map.50 = (bf16[16,2,64,1024]{3,2,1,0:T(8,128)(2,1)S(1)}, f32[16,4,16]{2,1,0:T(4,128)S(1)}) custom-call(bf16[1,8192,128]{2,1,0:T(8,128)(2,1)} %k_ref.1, bf16[1,8192,128]{2,1,0:T(8,128)(2,1)} %v_ref.1, bf16[1,8192]{1,0:T(2,128)(2,1)} %g_ref.1), custom_call_target="tpu_custom_call" | custom-call | tf_op jit(solution)/shard_map/pallas_call | solution.py:247
  58.2 2.3 %shard_map.51 = (bf16[16,64,2048]{2,1,0:T(8,128)(2,1)}, f32[16,4,16]{2,1,0:T(4,128)}) custom-call(bf16[16,2,64,1024]{3,2,1,0:T(8,128)(2,1)S(1)} %get-tuple-element.4.wide_ref, f32[16,4,16]{2,1,0:T(4,128)S(1)} %get-tuple-element.5.narrow_ref), custom_call_target="tpu_custom_call" | custom-call | tf_op jit(solution)/shard_map/pallas_call | solution.py:275

commit v7 on v6

--- a/solution.py
+++ b/solution.py
@@ -45,6 +45,7 @@
 
 ORDER = send_order()
 LINES = [o for o in ORDER if axes_used(o) <= 1]
+SAME_CORE = [o for o in LINES if o[3] == 0]
 PLANES = [o for o in ORDER if axes_used(o) == 2]
 REST = [o for o in ORDER if axes_used(o) == 3]
 
@@ -134,8 +135,8 @@
             device_id_type=MESH,
         ).start()
 
-    def greet(semaphore):
-        for offset in LINES:
+    def greet(semaphore, peers):
+        for offset in peers:
             pl.semaphore_signal(
                 semaphore, inc=1, device_id=target(offset), device_id_type=MESH
             )
@@ -154,7 +155,7 @@
     gain_copy = pltpu.make_async_copy(g_ref, gain, gain_sem)
     gain_copy.start()
     load(0)
-    greet(barrier)
+    greet(barrier, LINES)
     for chunk in range(1, AHEAD):
         load(chunk)
     rows_out[...] = jnp.zeros_like(rows_out)
@@ -163,15 +164,15 @@
     compute(1)
     done = 2
     pl.semaphore_wait(barrier, len(LINES))
-    greet(plane_sem)
+    greet(plane_sem, SAME_CORE)
     done = send_group(LINES, done)
-    pl.semaphore_wait(plane_sem, len(LINES))
-    greet(rest_sem)
+    pl.semaphore_wait(plane_sem, len(SAME_CORE))
+    greet(rest_sem, SAME_CORE)
     done = send_group(PLANES[:36], done)
     while done < len(CHUNKS):
         compute(done)
         done += 1
-    pl.semaphore_wait(rest_sem, len(LINES))
+    pl.semaphore_wait(rest_sem, len(SAME_CORE))
 
     def send_row(source, landing, there, other, stage):
         pltpu.make_async_remote_copy(

time: 60.7 us -> 60.1 us (level)
  no operation moved by 1% of the time
where the time goes in v7:
time: 60.1 us; the launch traced here: 59.9 us
  Pallas kernels  59.3 us (99%)
  between operations  0.64 us (1%)
    pallas_call x1, Pallas kernels, on_device(): pl.pallas_call(functools.partial(exchange, sections, ranks), out_shape=(p...  57 us
    pallas_call x1, Pallas kernels, on_device(): pl.pallas_call(settle, out_shape=(jax.ShapeDtypeStruct((sections, share,...  2.28 us

profile of v7, /device:TPU:1, one launch (start us, length us, event | category | flops | bytes accessed | tf_op | source)
XLA Modules:
  0.0 59.9 jit_solution(16513097119869574367)
XLA Ops:
  0.6 57.0 %shard_map.50 = (bf16[16,2,64,1024]{3,2,1,0:T(8,128)(2,1)S(1)}, f32[16,4,16]{2,1,0:T(4,128)S(1)}) custom-call(bf16[1,8192,128]{2,1,0:T(8,128)(2,1)} %k_ref.1, bf16[1,8192,128]{2,1,0:T(8,128)(2,1)} %v_ref.1, bf16[1,8192]{1,0:T(2,128)(2,1)} %g_ref.1), custom_call_target="tpu_custom_call" | custom-call | tf_op jit(solution)/shard_map/pallas_call | solution.py:248
  57.6 2.3 %shard_map.51 = (bf16[16,64,2048]{2,1,0:T(8,128)(2,1)}, f32[16,4,16]{2,1,0:T(4,128)}) custom-call(bf16[16,2,64,1024]{3,2,1,0:T(8,128)(2,1)S(1)} %get-tuple-element.4.wide_ref, f32[16,4,16]{2,1,0:T(4,128)S(1)} %get-tuple-element.5.narrow_ref), custom_call_target="tpu_custom_call" | custom-call | tf_op jit(solution)/shard_map/pallas_call | solution.py:276

commit v8 on v7

--- a/solution.py
+++ b/solution.py
@@ -45,7 +45,8 @@
 
 ORDER = send_order()
 LINES = [o for o in ORDER if axes_used(o) <= 1]
-SAME_CORE = [o for o in LINES if o[3] == 0]
+ALONG_YZ = [o for o in LINES if o[3] == 0 and o[0] == 0]
+ALONG_X = [o for o in LINES if o[3] == 0 and o[0] != 0]
 PLANES = [o for o in ORDER if axes_used(o) == 2]
 REST = [o for o in ORDER if axes_used(o) == 3]
 
@@ -164,15 +165,15 @@
     compute(1)
     done = 2
     pl.semaphore_wait(barrier, len(LINES))
-    greet(plane_sem, SAME_CORE)
+    greet(plane_sem, ALONG_YZ)
     done = send_group(LINES, done)
-    pl.semaphore_wait(plane_sem, len(SAME_CORE))
-    greet(rest_sem, SAME_CORE)
+    pl.semaphore_wait(plane_sem, len(ALONG_YZ))
+    greet(rest_sem, ALONG_X)
     done = send_group(PLANES[:36], done)
     while done < len(CHUNKS):
         compute(done)
         done += 1
-    pl.semaphore_wait(rest_sem, len(SAME_CORE))
+    pl.semaphore_wait(rest_sem, len(ALONG_X))
 
     def send_row(source, landing, there, other, stage):
         pltpu.make_async_remote_copy(

time: 60.1 us -> 60 us (level)
  no operation moved by 1% of the time
where the time goes in v8:
time: 60 us; the launch traced here: 59.9 us
  Pallas kernels  59.2 us (99%)
  between operations  0.64 us (1%)
    pallas_call x1, Pallas kernels, on_device(): pl.pallas_call(functools.partial(exchange, sections, ranks), out_shape=(p...  56.9 us
    pallas_call x1, Pallas kernels, on_device(): pl.pallas_call(settle, out_shape=(jax.ShapeDtypeStruct((sections, share,...  2.28 us

profile of v8, /device:TPU:1, one launch (start us, length us, event | category | flops | bytes accessed | tf_op | source)
XLA Modules:
  0.0 59.9 jit_solution(7720639829027257480)
XLA Ops:
  0.6 56.9 %shard_map.50 = (bf16[16,2,64,1024]{3,2,1,0:T(8,128)(2,1)S(1)}, f32[16,4,16]{2,1,0:T(4,128)S(1)}) custom-call(bf16[1,8192,128]{2,1,0:T(8,128)(2,1)} %k_ref.1, bf16[1,8192,128]{2,1,0:T(8,128)(2,1)} %v_ref.1, bf16[1,8192]{1,0:T(2,128)(2,1)} %g_ref.1), custom_call_target="tpu_custom_call" | custom-call | tf_op jit(solution)/shard_map/pallas_call | solution.py:249
  57.6 2.3 %shard_map.51 = (bf16[16,64,2048]{2,1,0:T(8,128)(2,1)}, f32[16,4,16]{2,1,0:T(4,128)}) custom-call(bf16[16,2,64,1024]{3,2,1,0:T(8,128)(2,1)S(1)} %get-tuple-element.4.wide_ref, f32[16,4,16]{2,1,0:T(4,128)S(1)} %get-tuple-element.5.narrow_ref), custom_call_target="tpu_custom_call" | custom-call | tf_op jit(solution)/shard_map/pallas_call | solution.py:277

commit v9 on v7

--- a/solution.py
+++ b/solution.py
@@ -46,6 +46,7 @@
 ORDER = send_order()
 LINES = [o for o in ORDER if axes_used(o) <= 1]
 SAME_CORE = [o for o in LINES if o[3] == 0]
+ALONG_X = [o for o in SAME_CORE if o[0] != 0]
 PLANES = [o for o in ORDER if axes_used(o) == 2]
 REST = [o for o in ORDER if axes_used(o) == 3]
 
@@ -167,12 +168,12 @@
     greet(plane_sem, SAME_CORE)
     done = send_group(LINES, done)
     pl.semaphore_wait(plane_sem, len(SAME_CORE))
-    greet(rest_sem, SAME_CORE)
+    greet(rest_sem, ALONG_X)
     done = send_group(PLANES[:36], done)
     while done < len(CHUNKS):
         compute(done)
         done += 1
-    pl.semaphore_wait(rest_sem, len(SAME_CORE))
+    pl.semaphore_wait(rest_sem, len(ALONG_X))
 
     def send_row(source, landing, there, other, stage):
         pltpu.make_async_remote_copy(

time: 60.1 us -> 60.1 us (level)
  no operation moved by 1% of the time
where the time goes in v9:
time: 60.1 us; the launch traced here: 59.9 us
  Pallas kernels  59.3 us (99%)
  between operations  0.64 us (1%)
    pallas_call x1, Pallas kernels, on_device(): pl.pallas_call(functools.partial(exchange, sections, ranks), out_shape=(p...  57 us
    pallas_call x1, Pallas kernels, on_device(): pl.pallas_call(settle, out_shape=(jax.ShapeDtypeStruct((sections, share,...  2.28 us

profile of v9, /device:TPU:1, one launch (start us, length us, event | category | flops | bytes accessed | tf_op | source)
XLA Modules:
  0.0 59.9 jit_solution(8989035199822469272)
XLA Ops:
  0.6 57.0 %shard_map.50 = (bf16[16,2,64,1024]{3,2,1,0:T(8,128)(2,1)S(1)}, f32[16,4,16]{2,1,0:T(4,128)S(1)}) custom-call(bf16[1,8192,128]{2,1,0:T(8,128)(2,1)} %k_ref.1, bf16[1,8192,128]{2,1,0:T(8,128)(2,1)} %v_ref.1, bf16[1,8192]{1,0:T(2,128)(2,1)} %g_ref.1), custom_call_target="tpu_custom_call" | custom-call | tf_op jit(solution)/shard_map/pallas_call | solution.py:249
  57.6 2.3 %shard_map.51 = (bf16[16,64,2048]{2,1,0:T(8,128)(2,1)}, f32[16,4,16]{2,1,0:T(4,128)}) custom-call(bf16[16,2,64,1024]{3,2,1,0:T(8,128)(2,1)S(1)} %get-tuple-element.4.wide_ref, f32[16,4,16]{2,1,0:T(4,128)S(1)} %get-tuple-element.5.narrow_ref), custom_call_target="tpu_custom_call" | custom-call | tf_op jit(solution)/shard_map/pallas_call | solution.py:277
